TPU v7x, 32 devices: a whole 2x2x4 slice. The times are simulated.
32 devices in a mesh: mem: 8 (over z, x), chan: 4 (over y, core).
Axes of the slice: x: 2, y: 2, z: 4, core: 2. Of those that a mesh axis runs over, the one named last changes fastest.
Arguments:
- state_anom: bfloat16 [8, 64, 137], P(None, 'mem'), may hold values from -6 to 6
- radiance_anom: bfloat16 [8, 64, 8704], P(None, 'mem', 'chan'), may hold values from -6 to 6
- inv_noise: float32 [8704], P('chan'), may hold values from 0.02 to 0.2
- innovation: float32 [8, 8704], P(None, 'chan'), may hold values from -6 to 6
- valid_count: int32 [8], replicated, may hold values from 4352 to 8461
Outputs:
- information: float32 [8, 137, 137], P('mem')
- gradient: float32 [8, 137], P('mem')
- increment: float32 [8, 137], P('mem')
All inputs are finite; a program needn't handle non-finite values.
Results may differ from a plain program's by a relative error of at most 0.0003.
Values may be sent and summed in bfloat16 or wider, within the bound.
A program may use at most 64 MiB of HBM per device.

v0:
```python
import functools
import jax
import jax.numpy as jnp
from jax import lax
from jax.experimental import pallas as pl
from jax.experimental.pallas import tpu as pltpu
from jax.sharding import PartitionSpec as P

F32, BF16 = jnp.float32, jnp.bfloat16
LANES, SUB = 128, 8
PARTS = 4
TINY = 2e-38
VMEM_LIMIT = 60 * 1024 * 1024


def up(x, to):
    return -(-x // to) * to


def split3(x):
    a = x.astype(BF16)
    rest = x - a.astype(F32)
    b = rest.astype(BF16)
    c = (rest - b.astype(F32)).astype(BF16)
    return a, b, c


def pieces(width, count):
    tiles = width // LANES
    marks = [(tiles - tiles * i // count) * LANES for i in range(count, 0, -1)] + [width]
    return list(zip(marks[:-1], marks[1:]))


def orthogonalise(anom, vectors_ref, lower_ref):
    total, states = anom.shape
    lanes = vectors_ref.shape[1]
    anom = jnp.concatenate([anom, jnp.zeros((total, lanes - states), F32)], 1)
    cid = lax.broadcasted_iota(jnp.int32, lower_ref.shape, 1)
    rid = lax.broadcasted_iota(jnp.int32, lower_ref.shape, 0)
    lower = jnp.zeros(lower_ref.shape, F32)
    for k in range(total):
        top = k // SUB * SUB
        live = anom[top:]
        vector = anom[k:k + 1]
        dots = jnp.sum(live * vector, axis=1, keepdims=True)
        norm = dots[k - top:k - top + 1]
        inverse = jnp.where(norm > TINY, 1.0 / norm, 0.0)
        after = lax.broadcasted_iota(jnp.int32, (total - top, 1), 0) > k - top
        live = live - jnp.where(after, dots * inverse, 0.0) * vector
        pad = [] if top == 0 else [jnp.zeros((top, 1), F32)]
        lower = jnp.where((cid == k) & (rid >= k), jnp.concatenate(pad + [dots], 0), lower)
        anom = live if top == 0 else jnp.concatenate([anom[:top], live], 0)
    diagonal = jnp.where(cid == rid, lower, 0.0)
    across = jnp.sum(diagonal, axis=0, keepdims=True)
    down = jnp.sum(diagonal, axis=1, keepdims=True)
    lower_ref[...] = lower * jnp.where(across > TINY, lax.rsqrt(across), 0.0)
    vectors_ref[...] = anom * jnp.where(down > TINY, lax.rsqrt(down), 0.0)


def gram_kernel(n_mem, n_chan, parts_of_slab, count_ref, state_ref, rad_ref, noise_ref, innov_ref,
                gram_ref, states_ref, *rest):
    basis_refs = rest[:-11]
    (held, held_states, innov, parts,
     local_sem, send_sem, recv_sem, ssend_sem, srecv_sem, psend_sem, precv_sem) = rest[-11:]
    me, slab = lax.axis_index("mem"), lax.axis_index("chan")
    members = rad_ref.shape[1]
    width = rad_ref.shape[2]
    total = n_mem * members
    columns = parts.shape[2]

    barrier = pltpu.get_barrier_semaphore()
    for k in range(1, n_mem):
        pl.semaphore_signal(barrier, inc=1, device_id={"mem": lax.rem(me + k, n_mem)})
    for k in range(1, n_chan):
        pl.semaphore_signal(barrier, inc=1, device_id={"chan": lax.rem(slab + k, n_chan)})
    own = [
        pltpu.make_async_copy(rad_ref.at[me], held.at[0], local_sem.at[0]),
        pltpu.make_async_copy(state_ref.at[me], held_states.at[0], local_sem.at[1]),
        pltpu.make_async_copy(innov_ref, innov, local_sem.at[2]),
    ]
    for copy in own:
        copy.start()
    for copy in own:
        copy.wait()
    slots = slab * width + lax.broadcasted_iota(jnp.int32, (1, width), 1)
    weight = jnp.where(slots < count_ref[me], noise_ref[...].reshape(1, width), 0.0)
    pull = weight * innov[pl.ds(me, 1), :]
    pull = [part.astype(F32) for part in split3(pull)]
    pl.semaphore_wait(barrier, n_mem - 1 + n_chan - 1)

    small = []
    for k in range(1, n_mem):
        peer = lax.rem(me + k, n_mem)
        small.append(pltpu.make_async_remote_copy(
            src_ref=state_ref.at[peer], dst_ref=held_states.at[k],
            send_sem=ssend_sem.at[k], recv_sem=srecv_sem.at[k], device_id={"mem": peer}))
        small[-1].start()
    cuts = pieces(width, parts_of_slab)
    sends, late = [], []
    for c, (lo, hi) in enumerate(cuts):
        for k in range(n_mem - 1, 0, -1):
            peer = lax.rem(me + k, n_mem)
            late.append(pltpu.make_async_remote_copy(
                src_ref=rad_ref.at[peer, :, lo:hi], dst_ref=held.at[k, :, lo:hi],
                send_sem=send_sem.at[c, k], recv_sem=recv_sem.at[c, k], device_id={"mem": peer}))
            late[-1].start()
        sends.append(late)
        late = []
    for copy in small:
        copy.wait_recv()
    states_ref[...] = held_states[...]
    if basis_refs:
        orthogonalise(held_states[...].astype(F32).reshape(total, held_states.shape[2]), *basis_refs)
    extra = columns - total
    row = lax.broadcasted_iota(jnp.int32, (extra, 1), 0)
    acc = jnp.zeros((total, columns), F32)
    step = 2 * LANES
    for (start, stop), copies in zip(cuts, sends):
        for copy in copies:
            copy.wait_recv()
        for lo in range(start, stop, step):
            hi = min(lo + step, stop)
            block = held[:, :, lo:hi].astype(F32).reshape(total, hi - lo)
            scaled = block * weight[:, lo:hi]
            first = scaled.astype(BF16)
            second = (scaled - first.astype(F32)).astype(BF16)
            p0, p1, p2 = (part[:, lo:hi] for part in pull)
            tail0 = jnp.where(row == 0, p0, jnp.where(row == 1, p2, 0.0)).astype(BF16)
            tail1 = jnp.where(row == 0, p1, 0.0).astype(BF16)
            block = block.astype(BF16)
            dims = (((1,), (1,)), ((), ()))
            acc += (
                lax.dot_general(block, jnp.concatenate([first, tail0], 0), dims, preferred_element_type=F32)
                + lax.dot_general(block, jnp.concatenate([second, tail1], 0), dims, preferred_element_type=F32)
            )
    parts[slab] = acc

    shares = []
    for k in range(1, n_chan):
        peer = lax.rem(slab + k, n_chan)
        shares.append(pltpu.make_async_remote_copy(
            src_ref=parts.at[slab], dst_ref=parts.at[slab],
            send_sem=psend_sem.at[k], recv_sem=precv_sem.at[k], device_id={"chan": peer}))
        shares[-1].start()
    for copy in small + sum(sends, []):
        copy.wait_send()
    for copy in shares:
        copy.wait()
    whole = parts[0]
    for k in range(1, n_chan):
        whole = whole + parts[k]
    gram_ref[...] = whole


def eliminate(system, order):
    rows, lanes = system.shape
    rid = lax.broadcasted_iota(jnp.int32, (SUB, LANES), 0)

    def wide(piece, tiles):
        return piece if tiles == 1 else jnp.concatenate([piece] * tiles, 1)

    for p in range(0, order, SUB):
        steps = min(SUB, order - p)
        base = p // LANES * LANES
        live = system[:, base:]
        tiles = (lanes - base) // LANES
        cols = []
        for j in range(steps):
            at = p - base + j
            full = jnp.broadcast_to(live[:, at:at + 1], (rows, LANES))
            cols.append([full[:p], full[p:p + SUB], full[p + SUB:]])
        block = live[p:p + SUB]
        above, below = live[:p], live[p + SUB:]
        for j in range(steps):
            inverse = 1.0 / cols[j][1][j:j + 1, :]
            pivot_row = block[j:j + 1, :] * wide(inverse, tiles)
            for later in range(j + 1, steps):
                c = cols[later]
                scale = c[1][j:j + 1, :] * inverse
                cols[later] = [
                    c[0] - cols[j][0] * scale if p else c[0],
                    jnp.where(rid == j, jnp.broadcast_to(scale, (SUB, LANES)), c[1] - cols[j][1] * scale),
                    c[2] - cols[j][2] * scale if p + SUB < rows else c[2],
                ]
            block = jnp.where(wide(rid, tiles) == j, jnp.broadcast_to(pivot_row, block.shape),
                              block - wide(cols[j][1], tiles) * pivot_row)
            if p:
                above = above - wide(cols[j][0], tiles) * pivot_row
            if p + SUB < rows:
                below = below - wide(cols[j][2], tiles) * pivot_row
        pieces = ([above] if p else []) + [block] + ([below] if p + SUB < rows else [])
        live = jnp.concatenate(pieces, 0) if len(pieces) > 1 else pieces[0]
        system = live if base == 0 else jnp.concatenate([system[:, :base], live], 1)
    return system[:, order:order + 1]


def solve_kernel(total, gram_ref, states_ref, *rest):
    basis_refs, (info_ref, grad_ref, inc_ref) = rest[:-3], rest[-3:]
    states = states_ref.shape[2]
    columns = gram_ref.shape[1]
    scale = 1.0 / (total - 1)
    rows, lanes = up(states, SUB), up(states + 1, LANES)
    anom = states_ref[...].astype(F32).reshape(total, states)
    anom = jnp.concatenate([anom, jnp.zeros((total, lanes - states), F32)], 1)
    gram = gram_ref[...]
    force = (gram[:, total:total + 1] + gram[:, total + 1:total + 2]) * scale
    grad_ref[...] = jnp.sum(force * anom, axis=0, keepdims=True)[:, :states]
    if basis_refs:
        vectors_ref, lower_ref = basis_refs
        lower = lower_ref[...]
        order = lower.T[:total]
        mixed = jnp.dot(order, gram, precision=lax.Precision.HIGHEST, preferred_element_type=F32)
        right = (mixed[:, total:total + 1] + mixed[:, total + 1:total + 2]) * scale
        full = jnp.concatenate([lower, jnp.zeros((columns - total, lower.shape[1]), F32)], 0)
        system = jnp.dot(mixed, full, precision=lax.Precision.HIGHEST, preferred_element_type=F32) * (scale * scale)
        rid = lax.broadcasted_iota(jnp.int32, system.shape, 0)
        cid = lax.broadcasted_iota(jnp.int32, system.shape, 1)
        system = system + jnp.where(rid == cid, 1.0, 0.0)
        system = jnp.where(cid == total, jnp.broadcast_to(right, system.shape), system)
        step = eliminate(system, total)
        inc_ref[...] = jnp.sum(step * vectors_ref[...], axis=0, keepdims=True)[:, :states]
    turned = anom.T[:rows].astype(BF16)
    anom = jnp.concatenate([anom, jnp.zeros((columns - total, lanes), F32)], 0).astype(BF16)
    half = functools.reduce(
        lambda a, b: b + a,
        [jnp.dot(turned, g, preferred_element_type=F32) for g in split3(gram)][::-1])
    grad = (half[:, total:total + 1] + half[:, total + 1:total + 2]) * scale
    info = functools.reduce(
        lambda a, b: b + a,
        [jnp.dot(h, anom, preferred_element_type=F32) for h in split3(half)][::-1])
    info = info * (scale * scale)
    info_ref[:, 0, :] = info[:states, :states]
    if basis_refs:
        return
    rid = lax.broadcasted_iota(jnp.int32, (rows, lanes), 0)
    cid = lax.broadcasted_iota(jnp.int32, (rows, lanes), 1)
    system = info + jnp.where(rid == cid, 1.0, 0.0)
    system = jnp.where(cid == states, jnp.broadcast_to(grad, (rows, lanes)), system)
    step = eliminate(system, states)
    lid = lax.broadcasted_iota(jnp.int32, (rows, LANES), 1)
    pair = jnp.where(lid == 1, step, 0.0)
    pair = jnp.concatenate([pair, jnp.zeros((lanes - rows, LANES), F32)], 0).T
    inc_ref[...] = pair[1:2, :states]


def shards(state_anom, radiance_anom, inv_noise, innovation, valid_count):
    n_mem, n_chan = lax.axis_size("mem"), lax.axis_size("chan")
    members, states = state_anom.shape[1:]
    width = radiance_anom.shape[2]
    total = members * n_mem
    columns = up(total + 16, LANES)
    vmem, anywhere = pl.BlockSpec(memory_space=pltpu.VMEM), pl.BlockSpec(memory_space=pl.ANY)
    dma = pltpu.SemaphoreType.DMA
    basis = () if total > states else (jax.ShapeDtypeStruct((total, up(states + 1, LANES)), F32),
                                       jax.ShapeDtypeStruct((total, up(total + 1, LANES)), F32))
    gram, own_states, *bases = pl.pallas_call(
        functools.partial(gram_kernel, n_mem, n_chan, PARTS),
        out_shape=(jax.ShapeDtypeStruct((total, columns), F32),
                   jax.ShapeDtypeStruct((n_mem, members, states), BF16)) + basis,
        in_specs=[pl.BlockSpec(memory_space=pltpu.SMEM), anywhere, anywhere, vmem, anywhere],
        out_specs=(vmem,) * (2 + len(basis)),
        scratch_shapes=[
            pltpu.VMEM((n_mem, members, width), BF16),
            pltpu.VMEM((n_mem, members, states), BF16),
            pltpu.VMEM(innovation.shape, F32),
            pltpu.VMEM((n_chan, total, columns), F32),
            dma((3,)), dma((PARTS, n_mem)), dma((PARTS, n_mem)), dma((n_mem,)), dma((n_mem,)),
            dma((n_chan,)), dma((n_chan,)),
        ],
        compiler_params=pltpu.CompilerParams(
            collective_id=0, has_side_effects=True, vmem_limit_bytes=VMEM_LIMIT),
    )(valid_count, state_anom, radiance_anom, inv_noise, innovation)
    information, gradient, increment = pl.pallas_call(
        functools.partial(solve_kernel, total),
        out_shape=(jax.ShapeDtypeStruct((states, 1, states), F32),
                   jax.ShapeDtypeStruct((1, states), F32),
                   jax.ShapeDtypeStruct((1, states), F32)),
        in_specs=[vmem] * (2 + len(basis)),
        out_specs=(vmem, vmem, vmem),
        compiler_params=pltpu.CompilerParams(vmem_limit_bytes=VMEM_LIMIT),
    )(gram, own_states, *bases)
    return information.transpose(1, 0, 2), gradient, increment


def solution(mesh):
    in_specs = (P(None, "mem", None), P(None, "mem", "chan"), P("chan"), P(None, "chan"), P())
    out_specs = (P("mem", None, None), P("mem", None), P("mem", None))
    return jax.shard_map(shards, mesh=mesh, in_specs=in_specs, out_specs=out_specs, check_vma=False)
```

profile of v0, /device:TPU:0, one launch (start us, length us, event | category | flops | bytes accessed | tf_op | source)
XLA Modules:
  0.0 25.9 jit_solution(2847903758203201730)
XLA Ops:
  0.6 21.8 %shard_map.76 = (f32[64,128]{1,0:T(8,128)}, bf16[8,8,137]{2,1,0:T(8,128)(2,1)}, f32[64,256]{1,0:T(8,128)}, f32[64,128]{1,0:T(8,128)}) custom-call(s32[8]{0:T(128)} %count_ref.1, bf16[8,8,137]{2,1,0:T(8,128)(2,1)} %state_ref.1, bf16[8,8,2176]{2,1,0:T(8,128)(2,1)} %rad_ref.1, f32[2176]{0:T(1024)} %noise_ref.1, f32[8,2176]{1,0:T(8,128)} %innov_ref.1), custom_call_target="tpu_custom_call" | custom-call | tf_op jit(solution)/shard_map/pallas_call | solution.py:256
  22.4 3.5 %shard_map.77 = (f32[137,1,137]{2,1,0:T(1,128)}, f32[1,137]{1,0:T(1,128)}, f32[1,137]{1,0:T(1,128)}) custom-call(f32[64,128]{1,0:T(8,128)} %get-tuple-element.10.gram_ref, bf16[8,8,137]{2,1,0:T(8,128)(2,1)} %get-tuple-element.11.states_ref, f32[64,256]{1,0:T(8,128)} %get-tuple-element.12.rest_0_, f32[64,128]{1,0:T(8,128)} %get-tuple-element.13.rest_1_), custom_call_target="tpu_custom_call" | custom-call | tf_op jit(solution)/shard_map/pallas_call | solution.py:273
where the time goes:
time: 26.2 us; the launch traced here: 25.9 us
  Pallas kernels  25.3 us (97%)
  between operations  0.64 us (2%)
    pallas_call x1, Pallas kernels, shards(): pl.pallas_call(functools.partial(gram_kernel, n_mem, n_chan, PARTS), out_...  21.8 us
    pallas_call x1, Pallas kernels, shards(): pl.pallas_call(functools.partial(solve_kernel, total), out_shape=(jax.Sha...  3.51 us

commit v1 on v0

v1 whole, which is shorter than its diff:
```python
import functools
import jax
import jax.numpy as jnp
from jax import lax
from jax.experimental import pallas as pl
from jax.experimental.pallas import tpu as pltpu
from jax.sharding import PartitionSpec as P

F32, BF16 = jnp.float32, jnp.bfloat16
LANES, SUB = 128, 8
PARTS = 4
STEP = 16
ROUNDING = 2.0 ** -20
MIB = 1024 * 1024


def up(x, to):
    return -(-x // to) * to


def split3(x):
    a = x.astype(BF16)
    rest = x - a.astype(F32)
    b = rest.astype(BF16)
    c = (rest - b.astype(F32)).astype(BF16)
    return a, b, c


def pieces(width, count):
    tiles = width // LANES
    marks = [(tiles - tiles * i // count) * LANES for i in range(count, 0, -1)] + [width]
    return list(zip(marks[:-1], marks[1:]))


def partner(me, k, n):
    if n & (n - 1):
        return lax.rem(me + k, n)
    other, bit = me, 1
    while bit < n:
        if k & bit:
            other = other + bit * (1 - 2 * lax.rem(me // bit, 2))
        bit *= 2
    return other


def cholesky_rows(square, total):
    lanes = square.shape[1]
    rid8 = lax.broadcasted_iota(jnp.int32, (SUB, lanes), 0)
    cid = lax.broadcasted_iota(jnp.int32, square.shape, 1)
    rid = lax.broadcasted_iota(jnp.int32, square.shape, 0)
    least = jnp.sum(jnp.where(cid == rid, square, 0.0), axis=1, keepdims=True) * ROUNDING
    least = jnp.broadcast_to(least, square.shape)
    live, upper = square, []
    for p in range(0, total, SUB):
        steps = min(SUB, total - p)
        cols = [jnp.broadcast_to(live[:, p + j:p + j + 1], live.shape) for j in range(steps)]
        block, below = live[:SUB], live[SUB:]
        rows = jnp.zeros((SUB, lanes), F32)
        for j in range(steps):
            pivot = cols[j][j:j + 1]
            inverse = jnp.where(pivot > least[p + j:p + j + 1], lax.rsqrt(pivot), 0.0)
            column = cols[j] * inverse
            row = block[j:j + 1] * inverse
            rows = jnp.where(rid8 == j, jnp.broadcast_to(row, rows.shape), rows)
            for later in range(j + 1, steps):
                cols[later] = cols[later] - column * (cols[later][j:j + 1] * inverse)
            block = block - column[:SUB] * row
            if p + SUB < total:
                below = below - column[SUB:] * row
        lane = lax.broadcasted_iota(jnp.int32, (SUB, lanes), 1)
        upper.append(jnp.where(lane >= rid8 + p, rows, 0.0))
        live = below
    return jnp.concatenate(upper, 0)


def gram_kernel(n_mem, n_chan, parts_of_slab, count_hbm, state_hbm, rad_hbm, noise_hbm, innov_hbm,
                gram_ref, states_ref, *rest):
    factor_refs = rest[:-12]
    (count, mine, mine_states, noise, innov, held, held_states, parts,
     local_sem, mem_sem, small_sem, chan_sem) = rest[-12:]
    me, slab = lax.axis_index("mem"), lax.axis_index("chan")
    members, width = rad_hbm.shape[1:]
    states = state_hbm.shape[2]
    total = n_mem * members
    half = total // 2
    columns = parts.shape[2]

    barrier = pltpu.get_barrier_semaphore()
    for k in range(1, n_mem):
        pl.semaphore_signal(barrier, inc=1, device_id={"mem": partner(me, k, n_mem)})
    for k in range(1, n_chan):
        pl.semaphore_signal(barrier, inc=1, device_id={"chan": partner(slab, k, n_chan)})
    local = [
        pltpu.make_async_copy(src, dst, local_sem.at[i])
        for i, (src, dst) in enumerate((
            (state_hbm, mine_states), (rad_hbm, mine), (state_hbm.at[me], held_states.at[0]),
            (rad_hbm.at[me], held.at[0]), (count_hbm, count), (noise_hbm, noise), (innov_hbm, innov)))
    ]
    for copy in local:
        copy.start()
    for copy in local[:2]:
        copy.wait()
    pl.semaphore_wait(barrier, n_mem - 1 + n_chan - 1)

    small = []
    for k in range(n_mem - 1, 0, -1):
        peer = partner(me, k, n_mem)
        small.append(pltpu.make_async_remote_copy(
            src_ref=mine_states.at[peer], dst_ref=held_states.at[k],
            send_sem=small_sem.at[0, k], recv_sem=small_sem.at[1, k], device_id={"mem": peer}))
        small[-1].start()
    cuts = pieces(width, parts_of_slab)
    sends = []
    for c, (lo, hi) in enumerate(cuts):
        batch = []
        for k in range(n_mem - 1, 0, -1):
            peer = partner(me, k, n_mem)
            batch.append(pltpu.make_async_remote_copy(
                src_ref=mine.at[peer, :, lo:hi], dst_ref=held.at[k, :, lo:hi],
                send_sem=mem_sem.at[0, c, k], recv_sem=mem_sem.at[1, c, k], device_id={"mem": peer}))
            batch[-1].start()
        sends.append(batch)
    for copy in local[2:]:
        copy.wait()
    slots = slab * width + lax.broadcasted_iota(jnp.int32, (1, width), 1)
    weight = jnp.where(slots < count[me], noise[...].reshape(1, width), 0.0)
    pull = weight * innov[pl.ds(me, 1), :]
    pull = [part.astype(F32) for part in split3(pull)]

    for copy in small:
        copy.wait_recv()
    states_ref[...] = held_states[...]
    if factor_refs:
        anom = held_states[...].astype(F32).reshape(total, states)
        anom = jnp.concatenate([anom, jnp.zeros((total, up(states, LANES) - states), F32)], 1)
        tall = jnp.concatenate([anom, jnp.zeros((up(total, LANES) - total, anom.shape[1]), F32)], 0)
        square = lax.dot_general(anom.astype(BF16), tall.astype(BF16), (((1,), (1,)), ((), ())),
                                 preferred_element_type=F32)
        factor_refs[0][...] = cholesky_rows(square, total)
    extra = columns - total - half
    row = lax.broadcasted_iota(jnp.int32, (extra, 1), 0)
    acc = jnp.zeros((total, columns), F32)
    step = 2 * LANES
    for (start, stop), copies in zip(cuts, sends):
        for copy in copies:
            copy.wait_recv()
        for lo in range(start, stop, step):
            hi = min(lo + step, stop)
            block = held[:, :, lo:hi].astype(F32).reshape(total, hi - lo)
            scaled = block * weight[:, lo:hi]
            first = scaled.astype(BF16)
            second = (scaled - first.astype(F32)).astype(BF16)
            p0, p1, p2 = (part[:, lo:hi] for part in pull)
            even = lax.rem(row, 2) == 0
            tail0 = jnp.where(row < 4, jnp.where(even, p0, p2), 0.0).astype(BF16)
            tail1 = jnp.where((row < 4) & even, p1, 0.0).astype(BF16)
            block = block.astype(BF16)
            dims = (((1,), (1,)), ((), ()))
            acc += (
                lax.dot_general(block, jnp.concatenate([first, first[half:], tail0], 0), dims,
                                preferred_element_type=F32)
                + lax.dot_general(block, jnp.concatenate([second, second[half:], tail1], 0), dims,
                                  preferred_element_type=F32)
            )
    lane = lax.broadcasted_iota(jnp.int32, (half, columns), 1)
    upper = (lane < total) | ((lane >= total + half) & (lane < total + half + 2))
    parts[slab] = jnp.where(upper, acc[:half], acc[half:])

    shares = []
    for k in range(1, n_chan):
        shares.append(pltpu.make_async_remote_copy(
            src_ref=parts.at[slab], dst_ref=parts.at[slab],
            send_sem=chan_sem.at[0, k], recv_sem=chan_sem.at[1, k],
            device_id={"chan": partner(slab, k, n_chan)}))
        shares[-1].start()
    for copy in small + sum(sends, []):
        copy.wait_send()
    for copy in shares:
        copy.wait()
    whole = parts[0]
    for k in range(1, n_chan):
        whole = whole + parts[k]
    gram_ref[...] = whole


def eliminate(system, order):
    rows, lanes = system.shape
    rid = lax.broadcasted_iota(jnp.int32, (SUB, LANES), 0)

    def wide(piece, tiles):
        return piece if tiles == 1 else jnp.concatenate([piece] * tiles, 1)

    for p in range(0, order, STEP):
        steps = min(STEP, order - p)
        size = up(steps, SUB)
        base = p // LANES * LANES
        tiles = (lanes - base) // LANES
        live = system[:, base:]
        at = p - base
        block = [live[p + i:p + i + SUB] for i in range(0, size, SUB)]
        cols = [[jnp.broadcast_to(b[:, at + j:at + j + 1], (SUB, LANES)) for b in block] for j in range(steps)]
        far = jnp.concatenate(([live[:p]] if p else []) + ([live[p + size:]] if p + size < rows else []), 0) \
            if size < rows else None
        for j in range(steps):
            home, k = divmod(j, SUB)
            inverse = 1.0 / cols[j][home][k:k + 1, :]
            pivot_row = block[home][k:k + 1, :] * wide(inverse, tiles)
            for later in range(j + 1, steps):
                c = cols[later]
                scale = c[home][k:k + 1, :] * inverse
                new = [c[i] - cols[j][i] * scale for i in range(len(c))]
                new[home] = jnp.where(rid == k, jnp.broadcast_to(scale, (SUB, LANES)), new[home])
                cols[later] = new
            new = [b - wide(cols[j][i], tiles) * pivot_row for i, b in enumerate(block)]
            new[home] = jnp.where(wide(rid, tiles) == k, jnp.broadcast_to(pivot_row, new[home].shape), new[home])
            block = new
        if far is not None:
            for j in range(steps):
                home, k = divmod(j, SUB)
                scale = jnp.broadcast_to(live_column(live, p, size, at + j), (rows - size, LANES))
                far = far - wide(scale, tiles) * block[home][k:k + 1, :]
        out = ([far[:p]] if p else []) + block + ([far[p:]] if p + size < rows else [])
        live = jnp.concatenate(out, 0) if len(out) > 1 else out[0]
        system = live if base == 0 else jnp.concatenate([system[:, :base], live], 1)
    return system[:, order:order + 1]


def live_column(live, p, size, at):
    rows = live.shape[0]
    column = ([live[:p, at:at + 1]] if p else []) + ([live[p + size:, at:at + 1]] if p + size < rows else [])
    return jnp.concatenate(column, 0) if len(column) > 1 else column[0]


def unfold(packed, total):
    half = total // 2
    top, last = packed[:, :total], packed[:, total:total + half]
    low = jnp.concatenate([top[:, half:].T, last], 1)
    first = total + half
    force = jnp.concatenate([packed[:, i:i + 1] + packed[:, i + 1:i + 2] for i in (first, first + 2)], 0)
    return jnp.concatenate([top, low], 0), force


def solve_kernel(total, gram_ref, states_ref, *rest):
    factor_refs, (info_ref, grad_ref, inc_ref) = rest[:-3], rest[-3:]
    states = states_ref.shape[2]
    scale = 1.0 / (total - 1)
    rows, lanes = up(states, SUB), up(states + 1, LANES)
    depth = up(total + 1, LANES)
    anom = states_ref[...].astype(F32).reshape(total, states)
    anom = jnp.concatenate([anom, jnp.zeros((total, lanes - states), F32)], 1)
    square, force = unfold(gram_ref[...], total)
    gram = jnp.concatenate([square, force, jnp.zeros((total, depth - total - 1), F32)], 1)
    gradient = jnp.sum((force * scale) * anom, axis=0, keepdims=True)
    grad_ref[...] = gradient[:, :states]
    deep = jnp.concatenate([anom, jnp.zeros((depth - total, lanes), F32)], 0).astype(BF16)
    if factor_refs:
        factor = factor_refs[0][...]
        mixed = jnp.dot(factor[:, :total], gram, precision=lax.Precision.HIGHEST, preferred_element_type=F32)
        full = jnp.concatenate([factor, jnp.zeros((depth - total, factor.shape[1]), F32)], 0)
        system = lax.dot_general(mixed, full, (((1,), (1,)), ((), ())), precision=lax.Precision.HIGHEST,
                                 preferred_element_type=F32) * (scale * scale)
        rid = lax.broadcasted_iota(jnp.int32, system.shape, 0)
        cid = lax.broadcasted_iota(jnp.int32, system.shape, 1)
        system = system + jnp.where(rid == cid, 1.0, 0.0)
        system = jnp.where(cid == total, mixed, system)
        moved = functools.reduce(
            lambda a, b: b + a,
            [jnp.dot(m, deep, preferred_element_type=F32) for m in split3(mixed)][::-1]) * (scale * scale * scale)
        step = eliminate(system, total)
        inc_ref[...] = (gradient - jnp.sum(step * moved, axis=0, keepdims=True))[:, :states]
    turned = anom.T[:rows].astype(BF16)
    half = functools.reduce(
        lambda a, b: b + a,
        [jnp.dot(turned, g, preferred_element_type=F32) for g in split3(gram)][::-1])
    grad = half[:, total:total + 1] * scale
    info = functools.reduce(
        lambda a, b: b + a,
        [jnp.dot(h, deep, preferred_element_type=F32) for h in split3(half)][::-1])
    info = info * (scale * scale)
    info_ref[:, 0, :] = info[:states, :states]
    if factor_refs:
        return
    rid = lax.broadcasted_iota(jnp.int32, (rows, lanes), 0)
    cid = lax.broadcasted_iota(jnp.int32, (rows, lanes), 1)
    system = info + jnp.where(rid == cid, 1.0, 0.0)
    system = jnp.where(cid == states, jnp.broadcast_to(grad, (rows, lanes)), system)
    step = eliminate(system, states)
    lid = lax.broadcasted_iota(jnp.int32, (rows, LANES), 1)
    pair = jnp.where(lid == 1, step, 0.0)
    pair = jnp.concatenate([pair, jnp.zeros((lanes - rows, LANES), F32)], 0).T
    inc_ref[...] = pair[1:2, :states]


def shards(state_anom, radiance_anom, inv_noise, innovation, valid_count):
    n_mem, n_chan = lax.axis_size("mem"), lax.axis_size("chan")
    members, states = state_anom.shape[1:]
    width = radiance_anom.shape[2]
    total = members * n_mem
    half = total // 2
    columns = up(total + half + 16, LANES)
    vmem, far = pl.BlockSpec(memory_space=pltpu.VMEM), pl.BlockSpec(memory_space=pltpu.HBM)
    dma = pltpu.SemaphoreType.DMA
    factor = () if total > states else (jax.ShapeDtypeStruct((total, up(total, LANES)), F32),)
    valid_count, state_anom, radiance_anom, inv_noise, innovation = (pltpu.with_memory_space_constraint(x, pltpu.HBM) for x in (valid_count, state_anom, radiance_anom, inv_noise, innovation))
    gram, own_states, *factors = pl.pallas_call(
        functools.partial(gram_kernel, n_mem, n_chan, PARTS),
        out_shape=(jax.ShapeDtypeStruct((half, columns), F32),
                   jax.ShapeDtypeStruct((n_mem, members, states), BF16)) + factor,
        in_specs=[far] * 5,
        out_specs=(vmem,) * (2 + len(factor)),
        scratch_shapes=[
            pltpu.SMEM(valid_count.shape, jnp.int32),
            pltpu.VMEM((n_mem, members, width), BF16),
            pltpu.VMEM((n_mem, members, states), BF16),
            pltpu.VMEM((width,), F32),
            pltpu.VMEM(innovation.shape, F32),
            pltpu.VMEM((n_mem, members, width), BF16),
            pltpu.VMEM((n_mem, members, states), BF16),
            pltpu.VMEM((n_chan, half, columns), F32),
            dma((7,)), dma((2, PARTS, n_mem)), dma((2, n_mem)), dma((2, n_chan)),
        ],
        compiler_params=pltpu.CompilerParams(
            collective_id=0, has_side_effects=True, vmem_limit_bytes=24 * MIB),
    )(valid_count, state_anom, radiance_anom, inv_noise, innovation)
    information, gradient, increment = pl.pallas_call(
        functools.partial(solve_kernel, total),
        out_shape=(jax.ShapeDtypeStruct((states, 1, states), F32),
                   jax.ShapeDtypeStruct((1, states), F32),
                   jax.ShapeDtypeStruct((1, states), F32)),
        in_specs=[vmem] * (2 + len(factor)),
        out_specs=(vmem, vmem, vmem),
        compiler_params=pltpu.CompilerParams(vmem_limit_bytes=24 * MIB),
    )(gram, own_states, *factors)
    return information.transpose(1, 0, 2), gradient, increment


def solution(mesh):
    in_specs = (P(None, "mem", None), P(None, "mem", "chan"), P("chan"), P(None, "chan"), P())
    out_specs = (P("mem", None, None), P("mem", None), P("mem", None))
    return jax.shard_map(shards, mesh=mesh, in_specs=in_specs, out_specs=out_specs, check_vma=False)
```

time: 26.2 us -> 21.3 us (0.81)
  Pallas kernels: 25.3 us -> 20.5 us
    pallas_call x1, Pallas kernels: 21.8 us -> 18 us  [shards(): pl.pallas_call(functools.partial(gram_kernel, n_mem, n_chan, PARTS), out_...]
    pallas_call x1, Pallas kernels: 3.51 us -> 2.49 us  [shards(): pl.pallas_call(functools.partial(solve_kernel, total), out_shape=(jax.Sha...]
where the time goes in v1:
time: 21.3 us; the launch traced here: 21.2 us
  Pallas kernels  20.5 us (96%)
  between operations  0.64 us (3%)
    pallas_call x1, Pallas kernels, shards(): pl.pallas_call(functools.partial(gram_kernel, n_mem, n_chan, PARTS), out_...  18 us
    pallas_call x1, Pallas kernels, shards(): pl.pallas_call(functools.partial(solve_kernel, total), out_shape=(jax.Sha...  2.49 us

profile of v1, /device:TPU:0, one launch (start us, length us, event | category | flops | bytes accessed | tf_op | source)
XLA Modules:
  0.0 21.2 jit_solution(2034368213039681714)
XLA Ops:
  0.6 18.0 %shard_map.76 = (f32[32,128]{1,0:T(8,128)S(1)}, bf16[8,8,137]{2,1,0:T(8,128)(2,1)S(1)}, f32[64,128]{1,0:T(8,128)S(1)}) custom-call(s32[8]{0:T(128)} %count_hbm.1, bf16[8,8,137]{2,1,0:T(8,128)(2,1)} %state_hbm.1, bf16[8,8,2176]{2,1,0:T(8,128)(2,1)} %rad_hbm.1, f32[2176]{0:T(1024)} %noise_hbm.1, f32[8,2176]{1,0:T(8,128)} %innov_hbm.1), custom_call_target="tpu_custom_call" | custom-call | tf_op jit(solution)/shard_map/pallas_call | solution.py:305
  18.7 2.5 %shard_map.77 = (f32[137,1,137]{2,1,0:T(1,128)}, f32[1,137]{1,0:T(1,128)}, f32[1,137]{1,0:T(1,128)}) custom-call(f32[32,128]{1,0:T(8,128)S(1)} %get-tuple-element.9.gram_ref, bf16[8,8,137]{2,1,0:T(8,128)(2,1)S(1)} %get-tuple-element.10.states_ref, f32[64,128]{1,0:T(8,128)S(1)} %get-tuple-element.11.rest_0_), custom_call_target="tpu_custom_call" | custom-call | tf_op jit(solution)/shard_map/pallas_call | solution.py:325

commit v2 on v1

--- a/solution.py
+++ b/solution.py
@@ -8,7 +8,7 @@
 
 F32, BF16 = jnp.float32, jnp.bfloat16
 LANES, SUB = 128, 8
-PARTS = 4
+PARTS = 3
 STEP = 16
 ROUNDING = 2.0 ** -20
 MIB = 1024 * 1024
@@ -37,8 +37,7 @@
         return lax.rem(me + k, n)
     other, bit = me, 1
     while bit < n:
-        if k & bit:
-            other = other + bit * (1 - 2 * lax.rem(me // bit, 2))
+        other = other + (k // bit % 2) * bit * (1 - 2 * (me // bit % 2))
         bit *= 2
     return other
 
@@ -75,9 +74,9 @@
 
 def gram_kernel(n_mem, n_chan, parts_of_slab, count_hbm, state_hbm, rad_hbm, noise_hbm, innov_hbm,
                 gram_ref, states_ref, *rest):
-    factor_refs = rest[:-12]
+    factor_refs = rest[:-14]
     (count, mine, mine_states, noise, innov, held, held_states, parts,
-     local_sem, mem_sem, small_sem, chan_sem) = rest[-12:]
+     local_sem, mem_sem, near_sem, far_sem, relay_sem, chan_sem) = rest[-14:]
     me, slab = lax.axis_index("mem"), lax.axis_index("chan")
     members, width = rad_hbm.shape[1:]
     states = state_hbm.shape[2]
@@ -93,8 +92,7 @@
     local = [
         pltpu.make_async_copy(src, dst, local_sem.at[i])
         for i, (src, dst) in enumerate((
-            (state_hbm, mine_states), (rad_hbm, mine), (state_hbm.at[me], held_states.at[0]),
-            (rad_hbm.at[me], held.at[0]), (count_hbm, count), (noise_hbm, noise), (innov_hbm, innov)))
+            (state_hbm, mine_states), (rad_hbm, mine), (count_hbm, count), (noise_hbm, noise), (innov_hbm, innov)))
     ]
     for copy in local:
         copy.start()
@@ -102,24 +100,36 @@
         copy.wait()
     pl.semaphore_wait(barrier, n_mem - 1 + n_chan - 1)
 
-    small = []
-    for k in range(n_mem - 1, 0, -1):
+    near = n_mem // 2
+    shared = near // n_chan if n_mem & (n_mem - 1) == 0 and near % n_chan == 0 else 0
+    direct = near if shared else n_mem
+
+    def state_copy(k, sems):
         peer = partner(me, k, n_mem)
-        small.append(pltpu.make_async_remote_copy(
+        return pltpu.make_async_remote_copy(
             src_ref=mine_states.at[peer], dst_ref=held_states.at[k],
-            send_sem=small_sem.at[0, k], recv_sem=small_sem.at[1, k], device_id={"mem": peer}))
-        small[-1].start()
+            send_sem=sems.at[0], recv_sem=sems.at[1], device_id={"mem": peer})
+
+    def blocks(source, target, sems):
+        return pltpu.make_async_remote_copy(
+            src_ref=source, dst_ref=target, send_sem=sems.at[0], recv_sem=sems.at[1],
+            device_id={"mem": partner(me, 1, n_mem)})
+
+    far = [state_copy(near + i * n_chan + slab, far_sem.at[i]) for i in range(shared)]
+    for copy in far:
+        copy.start()
+    for k in range(direct - 1, 0, -1):
+        state_copy(k, near_sem).start()
+    all_states = blocks(mine_states.at[1:direct], held_states.at[1:direct], near_sem)
     cuts = pieces(width, parts_of_slab)
     sends = []
     for c, (lo, hi) in enumerate(cuts):
-        batch = []
         for k in range(n_mem - 1, 0, -1):
             peer = partner(me, k, n_mem)
-            batch.append(pltpu.make_async_remote_copy(
+            pltpu.make_async_remote_copy(
                 src_ref=mine.at[peer, :, lo:hi], dst_ref=held.at[k, :, lo:hi],
-                send_sem=mem_sem.at[0, c, k], recv_sem=mem_sem.at[1, c, k], device_id={"mem": peer}))
-            batch[-1].start()
-        sends.append(batch)
+                send_sem=mem_sem.at[c, 0], recv_sem=mem_sem.at[c, 1], device_id={"mem": peer}).start()
+        sends.append(blocks(mine.at[1:, :, lo:hi], held.at[1:, :, lo:hi], mem_sem.at[c]))
     for copy in local[2:]:
         copy.wait()
     slots = slab * width + lax.broadcasted_iota(jnp.int32, (1, width), 1)
@@ -127,26 +137,30 @@
     pull = weight * innov[pl.ds(me, 1), :]
     pull = [part.astype(F32) for part in split3(pull)]
 
-    for copy in small:
+    relays = []
+    for i, copy in enumerate(far):
         copy.wait_recv()
-    states_ref[...] = held_states[...]
-    if factor_refs:
-        anom = held_states[...].astype(F32).reshape(total, states)
-        anom = jnp.concatenate([anom, jnp.zeros((total, up(states, LANES) - states), F32)], 1)
-        tall = jnp.concatenate([anom, jnp.zeros((up(total, LANES) - total, anom.shape[1]), F32)], 0)
-        square = lax.dot_general(anom.astype(BF16), tall.astype(BF16), (((1,), (1,)), ((), ())),
-                                 preferred_element_type=F32)
-        factor_refs[0][...] = cholesky_rows(square, total)
+        k = near + i * n_chan + slab
+        for j in range(1, n_chan):
+            pltpu.make_async_remote_copy(
+                src_ref=held_states.at[k], dst_ref=held_states.at[k], send_sem=relay_sem.at[0],
+                recv_sem=relay_sem.at[1], device_id={"chan": partner(slab, j, n_chan)}).start()
+    if shared:
+        size = shared * (n_chan - 1)
+        relays.append(blocks(mine_states.at[:size], held_states.at[:size], relay_sem))
+    def whole(own, others, lo, hi):
+        parts_of = [own[pl.ds(me, 1), :, lo:hi], others[1:, :, lo:hi]]
+        return jnp.concatenate([part.astype(F32).reshape(-1, hi - lo) for part in parts_of], 0)
+
     extra = columns - total - half
     row = lax.broadcasted_iota(jnp.int32, (extra, 1), 0)
     acc = jnp.zeros((total, columns), F32)
     step = 2 * LANES
-    for (start, stop), copies in zip(cuts, sends):
-        for copy in copies:
-            copy.wait_recv()
+    for (start, stop), copy in zip(cuts, sends):
+        copy.wait_recv()
         for lo in range(start, stop, step):
             hi = min(lo + step, stop)
-            block = held[:, :, lo:hi].astype(F32).reshape(total, hi - lo)
+            block = whole(mine, held, lo, hi)
             scaled = block * weight[:, lo:hi]
             first = scaled.astype(BF16)
             second = (scaled - first.astype(F32)).astype(BF16)
@@ -166,21 +180,29 @@
     upper = (lane < total) | ((lane >= total + half) & (lane < total + half + 2))
     parts[slab] = jnp.where(upper, acc[:half], acc[half:])
 
-    shares = []
     for k in range(1, n_chan):
-        shares.append(pltpu.make_async_remote_copy(
-            src_ref=parts.at[slab], dst_ref=parts.at[slab],
-            send_sem=chan_sem.at[0, k], recv_sem=chan_sem.at[1, k],
-            device_id={"chan": partner(slab, k, n_chan)}))
-        shares[-1].start()
-    for copy in small + sum(sends, []):
+        pltpu.make_async_remote_copy(
+            src_ref=parts.at[slab], dst_ref=parts.at[slab], send_sem=chan_sem.at[0], recv_sem=chan_sem.at[1],
+            device_id={"chan": partner(slab, k, n_chan)}).start()
+    all_states.wait_recv()
+    for copy in relays:
+        copy.wait_recv()
+    states_ref[pl.ds(0, 1)] = mine_states[pl.ds(me, 1)]
+    states_ref[1:] = held_states[1:]
+    if factor_refs:
+        anom = whole(mine_states, held_states, 0, states)
+        anom = jnp.concatenate([anom, jnp.zeros((total, up(states, LANES) - states), F32)], 1)
+        tall = jnp.concatenate([anom, jnp.zeros((up(total, LANES) - total, anom.shape[1]), F32)], 0)
+        square = lax.dot_general(anom.astype(BF16), tall.astype(BF16), (((1,), (1,)), ((), ())),
+                                 preferred_element_type=F32)
+        factor_refs[0][...] = cholesky_rows(square, total)
+    for copy in [all_states] + far + sends + relays:
         copy.wait_send()
-    for copy in shares:
-        copy.wait()
-    whole = parts[0]
+    blocks(parts.at[:n_chan - 1], parts.at[:n_chan - 1], chan_sem).wait()
+    summed = parts[0]
     for k in range(1, n_chan):
-        whole = whole + parts[k]
-    gram_ref[...] = whole
+        summed = summed + parts[k]
+    gram_ref[...] = summed
 
 
 def eliminate(system, order):
@@ -317,7 +339,7 @@
             pltpu.VMEM((n_mem, members, width), BF16),
             pltpu.VMEM((n_mem, members, states), BF16),
             pltpu.VMEM((n_chan, half, columns), F32),
-            dma((7,)), dma((2, PARTS, n_mem)), dma((2, n_mem)), dma((2, n_chan)),
+            dma((5,)), dma((PARTS, 2)), dma((2,)), dma((max(n_mem // 2 // n_chan, 1), 2)), dma((2,)), dma((2,)),
         ],
         compiler_params=pltpu.CompilerParams(
             collective_id=0, has_side_effects=True, vmem_limit_bytes=24 * MIB),

time: 21.3 us -> 20.1 us (0.944)
  Pallas kernels: 20.5 us -> 19.3 us
    pallas_call x1, Pallas kernels: 18 us -> 16.8 us  [shards(): pl.pallas_call(functools.partial(gram_kernel, n_mem, n_chan, PARTS), out_...]
where the time goes in v2:
time: 20.1 us; the launch traced here: 20 us
  Pallas kernels  19.3 us (96%)
  between operations  0.64 us (3%)
    pallas_call x1, Pallas kernels, shards(): pl.pallas_call(functools.partial(gram_kernel, n_mem, n_chan, PARTS), out_...  16.8 us
    pallas_call x1, Pallas kernels, shards(): pl.pallas_call(functools.partial(solve_kernel, total), out_shape=(jax.Sha...  2.49 us

profile of v2, /device:TPU:0, one launch (start us, length us, event | category | flops | bytes accessed | tf_op | source)
XLA Modules:
  0.0 20.0 jit_solution(11781436521260617573)
XLA Ops:
  0.6 16.8 %shard_map.76 = (f32[32,128]{1,0:T(8,128)S(1)}, bf16[8,8,137]{2,1,0:T(8,128)(2,1)S(1)}, f32[64,128]{1,0:T(8,128)S(1)}) custom-call(s32[8]{0:T(128)} %count_hbm.1, bf16[8,8,137]{2,1,0:T(8,128)(2,1)} %state_hbm.1, bf16[8,8,2176]{2,1,0:T(8,128)(2,1)} %rad_hbm.1, f32[2176]{0:T(1024)} %noise_hbm.1, f32[8,2176]{1,0:T(8,128)} %innov_hbm.1), custom_call_target="tpu_custom_call" | custom-call | tf_op jit(solution)/shard_map/pallas_call | solution.py:327
  17.5 2.5 %shard_map.77 = (f32[137,1,137]{2,1,0:T(1,128)}, f32[1,137]{1,0:T(1,128)}, f32[1,137]{1,0:T(1,128)}) custom-call(f32[32,128]{1,0:T(8,128)S(1)} %get-tuple-element.9.gram_ref, bf16[8,8,137]{2,1,0:T(8,128)(2,1)S(1)} %get-tuple-element.10.states_ref, f32[64,128]{1,0:T(8,128)S(1)} %get-tuple-element.11.rest_0_), custom_call_target="tpu_custom_call" | custom-call | tf_op jit(solution)/shard_map/pallas_call | solution.py:347

commit v3 on v2

v3 whole, which is shorter than its diff:
```python
import functools
import jax
import jax.numpy as jnp
from jax import lax
from jax.experimental import pallas as pl
from jax.experimental.pallas import tpu as pltpu
from jax.sharding import PartitionSpec as P

F32, BF16 = jnp.float32, jnp.bfloat16
LANES, SUB = 128, 8
PARTS = 1
STEP = 16
ROUNDING = 2.0 ** -20
MIB = 1024 * 1024


def up(x, to):
    return -(-x // to) * to


def split2(x):
    a = x.astype(BF16)
    return a, (x - a.astype(F32)).astype(BF16)


def split3(x):
    a = x.astype(BF16)
    return (a,) + split2(x - a.astype(F32))


def pieces(width, count):
    tiles = width // LANES
    marks = [(tiles - tiles * i // count) * LANES for i in range(count, 0, -1)] + [width]
    return list(zip(marks[:-1], marks[1:]))


def partner(me, k, n):
    if n & (n - 1):
        return lax.rem(me + k, n)
    other, bit = me, 1
    while bit < n:
        other = other + (k // bit % 2) * bit * (1 - 2 * (me // bit % 2))
        bit *= 2
    return other


def cholesky_rows(square, total):
    lanes = square.shape[1]
    rid8 = lax.broadcasted_iota(jnp.int32, (SUB, lanes), 0)
    cid = lax.broadcasted_iota(jnp.int32, square.shape, 1)
    rid = lax.broadcasted_iota(jnp.int32, square.shape, 0)
    least = jnp.sum(jnp.where(cid == rid, square, 0.0), axis=1, keepdims=True) * ROUNDING
    least = jnp.broadcast_to(least, square.shape)
    live, upper = square, []
    for p in range(0, total, SUB):
        steps = min(SUB, total - p)
        cols = [jnp.broadcast_to(live[:, p + j:p + j + 1], live.shape) for j in range(steps)]
        block, below = live[:SUB], live[SUB:]
        rows = jnp.zeros((SUB, lanes), F32)
        for j in range(steps):
            pivot = cols[j][j:j + 1]
            inverse = jnp.where(pivot > least[p + j:p + j + 1], lax.rsqrt(pivot), 0.0)
            column = cols[j] * inverse
            row = block[j:j + 1] * inverse
            rows = jnp.where(rid8 == j, jnp.broadcast_to(row, rows.shape), rows)
            for later in range(j + 1, steps):
                cols[later] = cols[later] - column * (cols[later][j:j + 1] * inverse)
            block = block - column[:SUB] * row
            if p + SUB < total:
                below = below - column[SUB:] * row
        lane = lax.broadcasted_iota(jnp.int32, (SUB, lanes), 1)
        upper.append(jnp.where(lane >= rid8 + p, rows, 0.0))
        live = below
    return jnp.concatenate(upper, 0)


def gram_kernel(n_mem, n_chan, parts_of_slab, count_hbm, state_hbm, rad_hbm, noise_hbm, innov_hbm,
                gram_ref, states_ref, *rest):
    factor_refs = rest[:-14]
    (count, mine, mine_states, noise, innov, held, held_states, parts,
     local_sem, mem_sem, near_sem, far_sem, relay_sem, chan_sem) = rest[-14:]
    me, slab = lax.axis_index("mem"), lax.axis_index("chan")
    members, width = rad_hbm.shape[1:]
    states = state_hbm.shape[2]
    total = n_mem * members
    columns = parts.shape[2]
    height = parts.shape[1] - SUB
    sent = height + (1 if columns == LANES else SUB)

    barrier = pltpu.get_barrier_semaphore()
    for k in range(1, n_mem):
        pl.semaphore_signal(barrier, inc=1, device_id={"mem": partner(me, k, n_mem)})
    for k in range(1, n_chan):
        pl.semaphore_signal(barrier, inc=1, device_id={"chan": partner(slab, k, n_chan)})
    local = [
        pltpu.make_async_copy(src, dst, local_sem.at[i])
        for i, (src, dst) in enumerate((
            (state_hbm, mine_states), (rad_hbm, mine), (count_hbm, count), (noise_hbm, noise), (innov_hbm, innov)))
    ]
    for copy in local:
        copy.start()
    for copy in local[:2]:
        copy.wait()
    pl.semaphore_wait(barrier, n_mem - 1 + n_chan - 1)

    near = n_mem // 2
    shared = near // n_chan if n_mem & (n_mem - 1) == 0 and near % n_chan == 0 else 0
    direct = near if shared else n_mem

    def state_copy(k, sems):
        peer = partner(me, k, n_mem)
        return pltpu.make_async_remote_copy(
            src_ref=mine_states.at[peer], dst_ref=held_states.at[k],
            send_sem=sems.at[0], recv_sem=sems.at[1], device_id={"mem": peer})

    def blocks(source, target, sems):
        return pltpu.make_async_remote_copy(
            src_ref=source, dst_ref=target, send_sem=sems.at[0], recv_sem=sems.at[1],
            device_id={"mem": partner(me, 1, n_mem)})

    far = [state_copy(near + i * n_chan + slab, far_sem.at[i]) for i in range(shared)]
    for copy in far:
        copy.start()
    for k in range(direct - 1, 0, -1):
        state_copy(k, near_sem).start()
    all_states = blocks(mine_states.at[1:direct], held_states.at[1:direct], near_sem)
    cuts = pieces(width, parts_of_slab)
    rounds = sorted(range(1, n_mem), key=lambda k: (k < near, k // 2 % 2, -k))
    sends = []
    for c, (lo, hi) in enumerate(cuts):
        for k in rounds:
            peer = partner(me, k, n_mem)
            pltpu.make_async_remote_copy(
                src_ref=mine.at[peer, :, lo:hi], dst_ref=held.at[k, :, lo:hi],
                send_sem=mem_sem.at[c, 0], recv_sem=mem_sem.at[c, 1], device_id={"mem": peer}).start()
        sends.append(blocks(mine.at[1:, :, lo:hi], held.at[1:, :, lo:hi], mem_sem.at[c]))
    for copy in local[2:]:
        copy.wait()
    slots = slab * width + lax.broadcasted_iota(jnp.int32, (1, width), 1)
    weight = jnp.where(slots < count[me], noise[...].reshape(1, width), 0.0)
    pull = weight * innov[pl.ds(me, 1), :]
    pull = [part.astype(F32) for part in split2(pull)]

    relays = []
    for i, copy in enumerate(far):
        copy.wait_recv()
        k = near + i * n_chan + slab
        for j in range(1, n_chan):
            pltpu.make_async_remote_copy(
                src_ref=held_states.at[k], dst_ref=held_states.at[k], send_sem=relay_sem.at[0],
                recv_sem=relay_sem.at[1], device_id={"chan": partner(slab, j, n_chan)}).start()
    if shared:
        size = shared * (n_chan - 1)
        relays.append(blocks(mine_states.at[:size], held_states.at[:size], relay_sem))
    def whole(own, others, lo, hi):
        parts_of = [own[pl.ds(me, 1), :, lo:hi], others[1:, :, lo:hi]]
        return jnp.concatenate([part.astype(F32).reshape(-1, hi - lo) for part in parts_of], 0)

    row = lax.broadcasted_iota(jnp.int32, (2 * SUB, 1), 0)
    acc = jnp.zeros((2 * total + 2 * SUB, columns), F32)
    step = 2 * LANES
    for (start, stop), copy in zip(cuts, sends):
        copy.wait_recv()
        for lo in range(start, stop, step):
            hi = min(lo + step, stop)
            block = whole(mine, held, lo, hi)
            first, second = split2(block * weight[:, lo:hi])
            tail = jnp.where(row == 0, pull[0][:, lo:hi], jnp.where(row == 1, pull[1][:, lo:hi], 0.0)).astype(BF16)
            block = jnp.concatenate([block.astype(BF16)] * (columns // total), 0)
            acc += lax.dot_general(jnp.concatenate([first, second, tail], 0), block, (((1,), (1,)), ((), ())),
                                   preferred_element_type=F32)
    square = acc[:total] + acc[total:2 * total]
    if columns > total:
        lane = lax.broadcasted_iota(jnp.int32, (height, columns), 1)
        square = jnp.where(lane < total, square[:height], square[height:])
    parts[slab, :height] = square
    parts[slab, height:] = jnp.broadcast_to(acc[2 * total:2 * total + 1] + acc[2 * total + 1:2 * total + 2],
                                            (SUB, columns))
    for k in range(1, n_chan):
        pltpu.make_async_remote_copy(
            src_ref=parts.at[slab, :sent], dst_ref=parts.at[slab, :sent], send_sem=chan_sem.at[0], recv_sem=chan_sem.at[1],
            device_id={"chan": partner(slab, k, n_chan)}).start()
    all_states.wait_recv()
    for copy in relays:
        copy.wait_recv()
    states_ref[pl.ds(0, 1)] = mine_states[pl.ds(me, 1)]
    states_ref[1:] = held_states[1:]
    if factor_refs:
        anom = whole(mine_states, held_states, 0, states)
        anom = jnp.concatenate([anom, jnp.zeros((total, up(states, LANES) - states), F32)], 1)
        tall = jnp.concatenate([anom, jnp.zeros((up(total, LANES) - total, anom.shape[1]), F32)], 0)
        square = lax.dot_general(anom.astype(BF16), tall.astype(BF16), (((1,), (1,)), ((), ())),
                                 preferred_element_type=F32)
        factor = cholesky_rows(square, total)
        factor_refs[0][...] = factor + pltpu.roll(factor, total, 1)
    for copy in [all_states] + far + sends + relays:
        copy.wait_send()
    arrived = parts.at[:n_chan - 1, :sent]
    blocks(arrived, arrived, chan_sem).wait()
    for rows in (slice(0, height), slice(height, height + 1)):
        summed = parts[0, rows]
        for k in range(1, n_chan):
            summed = summed + parts[k, rows]
        gram_ref[rows] = summed


def eliminate(system, order, right):
    rows, lanes = system.shape
    rid = lax.broadcasted_iota(jnp.int32, (SUB, LANES), 0)

    def wide(piece, tiles):
        return piece if tiles == 1 else jnp.concatenate([piece] * tiles, 1)

    for p in range(0, order, STEP):
        steps = min(STEP, order - p)
        size = up(steps, SUB)
        base = p // LANES * LANES
        tiles = (lanes - base) // LANES
        live = system[:, base:]
        at = p - base

        def others(x):
            kept = ([x[:p]] if p else []) + ([x[p + size:]] if p + size < rows else [])
            return (jnp.concatenate(kept, 0) if len(kept) > 1 else kept[0]) if kept else None

        def joined(inner, outer):
            out = ([outer[:p]] if p else []) + inner + ([outer[p:]] if p + size < rows else [])
            return jnp.concatenate(out, 0) if len(out) > 1 else out[0]

        block = [live[p + i:p + i + SUB] for i in range(0, size, SUB)]
        cols = [[jnp.broadcast_to(b[:, at + j:at + j + 1], (SUB, LANES)) for b in block] for j in range(steps)]
        cols.append([right[p + i:p + i + SUB] for i in range(0, size, SUB)])
        far, far_right = others(live), others(right)
        if far is not None:
            factors = [jnp.broadcast_to(far[:, at + j:at + j + 1], far_right.shape) for j in range(steps)]
        scales = [jnp.ones((SUB, LANES), F32)] * len(block)
        for j in range(steps):
            home, k = divmod(j, SUB)
            inverse = 1.0 / cols[j][home][k:k + 1, :]
            scales[home] = jnp.where(rid == k, inverse, scales[home])
            factor = list(cols[j])
            factor[home] = jnp.where(rid == k, 0.0, factor[home])
            for later in range(j + 1, steps + 1):
                c = cols[later]
                scale = c[home][k:k + 1, :] * inverse
                cols[later] = [c[i] - factor[i] * scale for i in range(len(c))]
            pivot_row = block[home][k:k + 1, :] * wide(inverse, tiles)
            block = [b - wide(factor[i], tiles) * pivot_row for i, b in enumerate(block)]
        block = [b * wide(s, tiles) for b, s in zip(block, scales)]
        solved = [c * s for c, s in zip(cols[steps], scales)]
        if far is not None:
            for j in range(steps):
                home, k = divmod(j, SUB)
                far = far - wide(factors[j], tiles) * block[home][k:k + 1, :]
                far_right = far_right - factors[j] * solved[home][k:k + 1, :]
        live = joined(block, far)
        right = joined(solved, far_right)
        system = live if base == 0 else jnp.concatenate([system[:, :base], live], 1)
    return right


def across(x, lane):
    return jnp.broadcast_to(x[:, lane:lane + 1], (x.shape[0], LANES))


def dots(*pairs):
    return functools.reduce(lambda a, b: a + b, [jnp.dot(a, b, preferred_element_type=F32) for a, b in pairs])


def solve_in_states(total, gram_ref, states_ref, info_ref, grad_ref, inc_ref):
    states = states_ref.shape[2]
    scale = 1.0 / (total - 1)
    rows, lanes = up(states, SUB), up(states, LANES)
    anom = states_ref[...].astype(F32).reshape(total, states)
    anom = jnp.concatenate([anom, jnp.zeros((total, lanes - states), F32)], 1)
    gram, force = gram_ref[:total], gram_ref[total:total + 1]
    gradient = jnp.dot(force, anom, precision=lax.Precision.HIGHEST, preferred_element_type=F32) * scale
    grad_ref[...] = gradient[:, :states]
    deep = anom.astype(BF16)
    turned = anom.T[:rows].astype(BF16)
    mixed = dots(*((turned, g) for g in split3(gram)[::-1]))
    info = dots(*((m, deep) for m in split3(mixed)[::-1])) * (scale * scale)
    info_ref[:, 0, :] = info[:states, :states]
    rid = lax.broadcasted_iota(jnp.int32, (rows, lanes), 0)
    cid = lax.broadcasted_iota(jnp.int32, (rows, lanes), 1)
    right = across(jnp.broadcast_to(gradient, (SUB, lanes)).T[:rows], 0)
    step = eliminate(info + jnp.where(rid == cid, 1.0, 0.0), states, right)
    if rows < lanes:
        step = jnp.concatenate([step, jnp.zeros((lanes - rows, LANES), F32)], 0)
    inc_ref[...] = step.T[:1, :states]


def solve_in_members(total, gram_ref, states_ref, factor_ref, info_ref, grad_ref, inc_ref):
    states = states_ref.shape[2]
    scale = 1.0 / (total - 1)
    rows, lanes = up(states, SUB), up(states, LANES)
    height = gram_ref.shape[0] - SUB
    packed, force = gram_ref[:height], gram_ref[height:height + 1]
    low = lax.broadcasted_iota(jnp.int32, packed.shape, 1) < total
    rolled = pltpu.roll(packed, total, 1)
    gram = jnp.concatenate([jnp.where(low, packed, rolled), jnp.where(low, rolled, packed)], 0)
    left = lax.broadcasted_iota(jnp.int32, (total, LANES), 1) < total
    factor = factor_ref[...]
    right = jnp.sum(jnp.where(left, factor * force, 0.0), axis=1, keepdims=True)
    right = jnp.broadcast_to(right, factor.shape)

    u0, u1, u2 = split3(factor)
    g0, g1, g2 = split3(gram)
    mixed = dots((jnp.concatenate([u0, u1], 1), jnp.concatenate([g0, g1, g0, g1], 0)),
                 (jnp.where(left, u0, u2), jnp.concatenate([g2, g0], 0)))
    m0, m1, m2 = split3(mixed)
    pad = jnp.zeros((LANES - total, LANES), BF16)
    pair = jnp.concatenate([jnp.where(left, u0, u1), pad], 0)
    last = jnp.concatenate([jnp.where(left, u2, u0), pad], 0)
    dims = (((1,), (1,)), ((), ()))
    system = (lax.dot_general(jnp.concatenate([m0, m1], 1), jnp.concatenate([pair, pair], 1), dims,
                              preferred_element_type=F32)
              + lax.dot_general(jnp.where(left, m0, m2), last, dims, preferred_element_type=F32)) * (scale * scale)
    rid = lax.broadcasted_iota(jnp.int32, system.shape, 0)
    cid = lax.broadcasted_iota(jnp.int32, system.shape, 1)
    step = eliminate(system + jnp.where(rid == cid, 1.0, 0.0), total, right)

    anom = states_ref[...].astype(F32).reshape(total, states)
    anom = jnp.concatenate([anom, jnp.zeros((total, lanes - states), F32)], 1)
    twice = jnp.concatenate([anom, anom], 0)
    once = jnp.concatenate([anom, jnp.zeros_like(anom)], 0).astype(BF16)
    f0, f1, f2 = split3(jnp.broadcast_to(force, (2 * SUB, LANES)))
    gradient = (dots((f2, once), (jnp.where(left[:2 * SUB], f0, f1), twice.astype(BF16))) * scale)[:1]
    grad_ref[...] = gradient[:, :states]
    moved = dots((m2, once), (jnp.where(left, m0, m1), twice.astype(BF16))) * (scale * scale * scale)
    inc_ref[...] = (gradient - jnp.sum(jnp.concatenate([step] * (lanes // LANES), 1) * moved,
                                       axis=0, keepdims=True))[:, :states]
    across_states = twice.T[:rows].astype(BF16)
    outer = dots((across_states, jnp.concatenate([g2, jnp.zeros_like(g2)], 0)),
                 (across_states, jnp.concatenate([g0, g1], 0)))
    h0, h1, h2 = split3(outer)
    left = lax.broadcasted_iota(jnp.int32, outer.shape, 1) < total
    info = dots((h2, once), (jnp.where(left, h0, h1), twice.astype(BF16))) * (scale * scale)
    info_ref[:, 0, :] = info[:states, :states]


def shards(state_anom, radiance_anom, inv_noise, innovation, valid_count):
    n_mem, n_chan = lax.axis_size("mem"), lax.axis_size("chan")
    members, states = state_anom.shape[1:]
    width = radiance_anom.shape[2]
    total = members * n_mem
    in_members = total <= states and 2 * total == LANES
    columns = LANES if in_members else total
    height = total * total // columns
    vmem, far = pl.BlockSpec(memory_space=pltpu.VMEM), pl.BlockSpec(memory_space=pltpu.HBM)
    dma = pltpu.SemaphoreType.DMA
    factor = () if not in_members else (jax.ShapeDtypeStruct((total, up(total, LANES)), F32),)
    valid_count, state_anom, radiance_anom, inv_noise, innovation = (pltpu.with_memory_space_constraint(x, pltpu.HBM) for x in (valid_count, state_anom, radiance_anom, inv_noise, innovation))
    gram, own_states, *factors = pl.pallas_call(
        functools.partial(gram_kernel, n_mem, n_chan, PARTS),
        out_shape=(jax.ShapeDtypeStruct((height + SUB, columns), F32),
                   jax.ShapeDtypeStruct((n_mem, members, states), BF16)) + factor,
        in_specs=[far] * 5,
        out_specs=(vmem,) * (2 + len(factor)),
        scratch_shapes=[
            pltpu.SMEM(valid_count.shape, jnp.int32),
            pltpu.VMEM((n_mem, members, width), BF16),
            pltpu.VMEM((n_mem, members, states), BF16),
            pltpu.VMEM((width,), F32),
            pltpu.VMEM(innovation.shape, F32),
            pltpu.VMEM((n_mem, members, width), BF16),
            pltpu.VMEM((n_mem, members, states), BF16),
            pltpu.VMEM((n_chan, height + SUB, columns), F32),
            dma((5,)), dma((PARTS, 2)), dma((2,)), dma((max(n_mem // 2 // n_chan, 1), 2)), dma((2,)), dma((2,)),
        ],
        compiler_params=pltpu.CompilerParams(
            collective_id=0, has_side_effects=True, vmem_limit_bytes=24 * MIB),
    )(valid_count, state_anom, radiance_anom, inv_noise, innovation)
    information, gradient, increment = pl.pallas_call(
        functools.partial(solve_in_members if in_members else solve_in_states, total),
        out_shape=(jax.ShapeDtypeStruct((states, 1, states), F32),
                   jax.ShapeDtypeStruct((1, states), F32),
                   jax.ShapeDtypeStruct((1, states), F32)),
        in_specs=[vmem] * (2 + len(factor)),
        out_specs=(vmem, vmem, vmem),
        compiler_params=pltpu.CompilerParams(vmem_limit_bytes=24 * MIB),
    )(gram, own_states, *factors)
    return information.transpose(1, 0, 2), gradient, increment


def solution(mesh):
    in_specs = (P(None, "mem", None), P(None, "mem", "chan"), P("chan"), P(None, "chan"), P())
    out_specs = (P("mem", None, None), P("mem", None), P("mem", None))
    return jax.shard_map(shards, mesh=mesh, in_specs=in_specs, out_specs=out_specs, check_vma=False)
```

time: 20.1 us -> 18.5 us (0.920)
  Pallas kernels: 19.3 us -> 17.7 us
    pallas_call x1, Pallas kernels: 16.8 us -> 15.6 us  [shards(): pl.pallas_call(functools.partial(gram_kernel, n_mem, n_chan, PARTS), out_...]
    pallas_call x1, Pallas kernels: 2.49 us -> 2.17 us  [shards(): pl.pallas_call(functools.partial(solve_in_members if in_members else solv...]
where the time goes in v3:
time: 18.5 us; the launch traced here: 18.4 us
  Pallas kernels  17.7 us (96%)
  between operations  0.64 us (3%)
    pallas_call x1, Pallas kernels, shards(): pl.pallas_call(functools.partial(gram_kernel, n_mem, n_chan, PARTS), out_...  15.6 us
    pallas_call x1, Pallas kernels, shards(): pl.pallas_call(functools.partial(solve_in_members if in_members else solv...  2.17 us

profile of v3, /device:TPU:0, one launch (start us, length us, event | category | flops | bytes accessed | tf_op | source)
XLA Modules:
  0.0 18.4 jit_solution(11868769355759576138)
XLA Ops:
  0.6 15.6 %shard_map.76 = (f32[40,128]{1,0:T(8,128)S(1)}, bf16[8,8,137]{2,1,0:T(8,128)(2,1)S(1)}, f32[64,128]{1,0:T(8,128)S(1)}) custom-call(s32[8]{0:T(128)} %count_hbm.1, bf16[8,8,137]{2,1,0:T(8,128)(2,1)} %state_hbm.1, bf16[8,8,2176]{2,1,0:T(8,128)(2,1)} %rad_hbm.1, f32[2176]{0:T(1024)} %noise_hbm.1, f32[8,2176]{1,0:T(8,128)} %innov_hbm.1), custom_call_target="tpu_custom_call" | custom-call | tf_op jit(solution)/shard_map/pallas_call | solution.py:354
  16.2 2.2 %shard_map.77 = (f32[137,1,137]{2,1,0:T(1,128)}, f32[1,137]{1,0:T(1,128)}, f32[1,137]{1,0:T(1,128)}) custom-call(f32[40,128]{1,0:T(8,128)S(1)} %get-tuple-element.9.gram_ref, bf16[8,8,137]{2,1,0:T(8,128)(2,1)S(1)} %get-tuple-element.10.states_ref, f32[64,128]{1,0:T(8,128)S(1)} %get-tuple-element.11.factor_ref), custom_call_target="tpu_custom_call" | custom-call | tf_op jit(solution)/shard_map/pallas_call | solution.py:374

commit v4 on v3

--- a/solution.py
+++ b/solution.py
@@ -74,6 +74,23 @@
     return jnp.concatenate(upper, 0)
 
 
+def stack_factor(factor, total):
+    u0, u1, u2 = (piece.astype(F32) for piece in split3(factor))
+    slot = lax.broadcasted_iota(jnp.int32, factor.shape, 1) // (total // 2)
+
+    def placed(*those):
+        out = []
+        for side in range(2):
+            tile = jnp.zeros(factor.shape, F32)
+            for i, piece in enumerate(those):
+                shift = (i - side) * (total // 2) % LANES
+                tile = jnp.where(slot == i, pltpu.roll(piece, shift, 1) if shift else piece, tile)
+            out.append(tile)
+        return jnp.concatenate(out, 0)
+
+    return placed(u0, u0, u1, u1), placed(u0, u2)
+
+
 def gram_kernel(n_mem, n_chan, parts_of_slab, count_hbm, state_hbm, rad_hbm, noise_hbm, innov_hbm,
                 gram_ref, states_ref, *rest):
     factor_refs = rest[:-14]
@@ -88,16 +105,22 @@
     sent = height + (1 if columns == LANES else SUB)
 
     barrier = pltpu.get_barrier_semaphore()
-    for k in range(1, n_mem):
-        pl.semaphore_signal(barrier, inc=1, device_id={"mem": partner(me, k, n_mem)})
-    for k in range(1, n_chan):
-        pl.semaphore_signal(barrier, inc=1, device_id={"chan": partner(slab, k, n_chan)})
+    def greet(rounds):
+        for k in rounds:
+            pl.semaphore_signal(barrier, inc=1, device_id={"mem": partner(me, k, n_mem)})
+
     local = [
         pltpu.make_async_copy(src, dst, local_sem.at[i])
         for i, (src, dst) in enumerate((
             (state_hbm, mine_states), (rad_hbm, mine), (count_hbm, count), (noise_hbm, noise), (innov_hbm, innov)))
     ]
-    for copy in local:
+    greet(range(n_mem - 1, n_mem // 2 - 1, -1))
+    local[0].start()
+    local[1].start()
+    greet(range(n_mem // 2 - 1, 0, -1))
+    for k in range(1, n_chan):
+        pl.semaphore_signal(barrier, inc=1, device_id={"chan": partner(slab, k, n_chan)})
+    for copy in local[2:]:
         copy.start()
     for copy in local[:2]:
         copy.wait()
@@ -193,6 +216,9 @@
                                  preferred_element_type=F32)
         factor = cholesky_rows(square, total)
         factor_refs[0][...] = factor + pltpu.roll(factor, total, 1)
+        stacked = stack_factor(factor, total)
+        for i, tile in enumerate(stacked):
+            factor_refs[1][:, i * LANES:(i + 1) * LANES] = tile
     for copy in [all_states] + far + sends + relays:
         copy.wait_send()
     arrived = parts.at[:n_chan - 1, :sent]
@@ -204,7 +230,7 @@
         gram_ref[rows] = summed
 
 
-def eliminate(system, order, right):
+def eliminate(system, order):
     rows, lanes = system.shape
     rid = lax.broadcasted_iota(jnp.int32, (SUB, LANES), 0)
 
@@ -218,6 +244,7 @@
         tiles = (lanes - base) // LANES
         live = system[:, base:]
         at = p - base
+        final = p + STEP >= order
 
         def others(x):
             kept = ([x[:p]] if p else []) + ([x[p + size:]] if p + size < rows else [])
@@ -229,10 +256,12 @@
 
         block = [live[p + i:p + i + SUB] for i in range(0, size, SUB)]
         cols = [[jnp.broadcast_to(b[:, at + j:at + j + 1], (SUB, LANES)) for b in block] for j in range(steps)]
-        cols.append([right[p + i:p + i + SUB] for i in range(0, size, SUB)])
-        far, far_right = others(live), others(right)
+        if final:
+            cols.append([across(b, order - base) for b in block])
+        far = others(live)
         if far is not None:
-            factors = [jnp.broadcast_to(far[:, at + j:at + j + 1], far_right.shape) for j in range(steps)]
+            factors = [across(far, at + j) for j in range(steps)]
+            far_right = across(far, order - base) if final else None
         scales = [jnp.ones((SUB, LANES), F32)] * len(block)
         for j in range(steps):
             home, k = divmod(j, SUB)
@@ -240,23 +269,24 @@
             scales[home] = jnp.where(rid == k, inverse, scales[home])
             factor = list(cols[j])
             factor[home] = jnp.where(rid == k, 0.0, factor[home])
-            for later in range(j + 1, steps + 1):
+            for later in range(j + 1, len(cols)):
                 c = cols[later]
                 scale = c[home][k:k + 1, :] * inverse
                 cols[later] = [c[i] - factor[i] * scale for i in range(len(c))]
             pivot_row = block[home][k:k + 1, :] * wide(inverse, tiles)
             block = [b - wide(factor[i], tiles) * pivot_row for i, b in enumerate(block)]
+        if final:
+            solved = [c * s for c, s in zip(cols[steps], scales)]
+            if far is not None:
+                terms = [factors[j] * solved[j // SUB][j % SUB:j % SUB + 1, :] for j in range(steps)]
+                far_right = far_right - sum(sum(terms[i::4][1:], terms[i]) for i in range(min(4, steps)))
+            return joined(solved, far_right)
         block = [b * wide(s, tiles) for b, s in zip(block, scales)]
-        solved = [c * s for c, s in zip(cols[steps], scales)]
         if far is not None:
             for j in range(steps):
-                home, k = divmod(j, SUB)
-                far = far - wide(factors[j], tiles) * block[home][k:k + 1, :]
-                far_right = far_right - factors[j] * solved[home][k:k + 1, :]
+                far = far - wide(factors[j], tiles) * block[j // SUB][j % SUB:j % SUB + 1, :]
         live = joined(block, far)
-        right = joined(solved, far_right)
         system = live if base == 0 else jnp.concatenate([system[:, :base], live], 1)
-    return right
 
 
 def across(x, lane):
@@ -270,7 +300,7 @@
 def solve_in_states(total, gram_ref, states_ref, info_ref, grad_ref, inc_ref):
     states = states_ref.shape[2]
     scale = 1.0 / (total - 1)
-    rows, lanes = up(states, SUB), up(states, LANES)
+    rows, lanes = up(states, SUB), up(states + 1, LANES)
     anom = states_ref[...].astype(F32).reshape(total, states)
     anom = jnp.concatenate([anom, jnp.zeros((total, lanes - states), F32)], 1)
     gram, force = gram_ref[:total], gram_ref[total:total + 1]
@@ -283,14 +313,14 @@
     info_ref[:, 0, :] = info[:states, :states]
     rid = lax.broadcasted_iota(jnp.int32, (rows, lanes), 0)
     cid = lax.broadcasted_iota(jnp.int32, (rows, lanes), 1)
-    right = across(jnp.broadcast_to(gradient, (SUB, lanes)).T[:rows], 0)
-    step = eliminate(info + jnp.where(rid == cid, 1.0, 0.0), states, right)
+    wide_right = jnp.broadcast_to(jnp.broadcast_to(gradient, (SUB, lanes)).T[:rows, :1], (rows, lanes))
+    step = eliminate(jnp.where(cid == states, wide_right, info + jnp.where(rid == cid, 1.0, 0.0)), states)
     if rows < lanes:
         step = jnp.concatenate([step, jnp.zeros((lanes - rows, LANES), F32)], 0)
     inc_ref[...] = step.T[:1, :states]
 
 
-def solve_in_members(total, gram_ref, states_ref, factor_ref, info_ref, grad_ref, inc_ref):
+def solve_in_members(total, gram_ref, states_ref, factor_ref, stacked_ref, info_ref, grad_ref, inc_ref):
     states = states_ref.shape[2]
     scale = 1.0 / (total - 1)
     rows, lanes = up(states, SUB), up(states, LANES)
@@ -306,19 +336,19 @@
 
     u0, u1, u2 = split3(factor)
     g0, g1, g2 = split3(gram)
-    mixed = dots((jnp.concatenate([u0, u1], 1), jnp.concatenate([g0, g1, g0, g1], 0)),
-                 (jnp.where(left, u0, u2), jnp.concatenate([g2, g0], 0)))
-    m0, m1, m2 = split3(mixed)
+    p0, p1, p2 = split3(packed)
+    deep = jnp.concatenate([p0, p1, p0, p1, p2, p0, jnp.zeros((2 * LANES - 6 * height, LANES), BF16)], 0)
+    halves = jnp.dot(stacked_ref[...].astype(BF16), deep, preferred_element_type=F32)
+    m0, m1, m2 = split3(jnp.where(left, halves[:total], halves[total:]))
     pad = jnp.zeros((LANES - total, LANES), BF16)
-    pair = jnp.concatenate([jnp.where(left, u0, u1), pad], 0)
-    last = jnp.concatenate([jnp.where(left, u2, u0), pad], 0)
     dims = (((1,), (1,)), ((), ()))
-    system = (lax.dot_general(jnp.concatenate([m0, m1], 1), jnp.concatenate([pair, pair], 1), dims,
-                              preferred_element_type=F32)
-              + lax.dot_general(jnp.where(left, m0, m2), last, dims, preferred_element_type=F32)) * (scale * scale)
+    system = sum(
+        lax.dot_general(jnp.concatenate(a, 1), jnp.concatenate([jnp.concatenate(b, 1), jnp.concatenate([pad, pad], 1)], 0),
+                        dims, preferred_element_type=F32)
+        for a, b in (((m0, m2), (u2, u0)), ((m0, m1), (u1, u1)), ((m0, m1), (u0, u0)))) * (scale * scale)
     rid = lax.broadcasted_iota(jnp.int32, system.shape, 0)
     cid = lax.broadcasted_iota(jnp.int32, system.shape, 1)
-    step = eliminate(system + jnp.where(rid == cid, 1.0, 0.0), total, right)
+    step = eliminate(jnp.where(cid == total, right, system + jnp.where(rid == cid, 1.0, 0.0)), total)
 
     anom = states_ref[...].astype(F32).reshape(total, states)
     anom = jnp.concatenate([anom, jnp.zeros((total, lanes - states), F32)], 1)
@@ -327,15 +357,15 @@
     f0, f1, f2 = split3(jnp.broadcast_to(force, (2 * SUB, LANES)))
     gradient = (dots((f2, once), (jnp.where(left[:2 * SUB], f0, f1), twice.astype(BF16))) * scale)[:1]
     grad_ref[...] = gradient[:, :states]
-    moved = dots((m2, once), (jnp.where(left, m0, m1), twice.astype(BF16))) * (scale * scale * scale)
+    moved = dots(*((m, twice.astype(BF16)) for m in (m2, m1, m0))) * (scale * scale * scale)
     inc_ref[...] = (gradient - jnp.sum(jnp.concatenate([step] * (lanes // LANES), 1) * moved,
                                        axis=0, keepdims=True))[:, :states]
     across_states = twice.T[:rows].astype(BF16)
     outer = dots((across_states, jnp.concatenate([g2, jnp.zeros_like(g2)], 0)),
                  (across_states, jnp.concatenate([g0, g1], 0)))
-    h0, h1, h2 = split3(outer)
+    h0, h1, h2 = split3(outer * (scale * scale))
     left = lax.broadcasted_iota(jnp.int32, outer.shape, 1) < total
-    info = dots((h2, once), (jnp.where(left, h0, h1), twice.astype(BF16))) * (scale * scale)
+    info = dots((h2, once), (jnp.where(left, h0, h1), twice.astype(BF16)))
     info_ref[:, 0, :] = info[:states, :states]
 
 
@@ -349,7 +379,8 @@
     height = total * total // columns
     vmem, far = pl.BlockSpec(memory_space=pltpu.VMEM), pl.BlockSpec(memory_space=pltpu.HBM)
     dma = pltpu.SemaphoreType.DMA
-    factor = () if not in_members else (jax.ShapeDtypeStruct((total, up(total, LANES)), F32),)
+    factor = () if not in_members else (jax.ShapeDtypeStruct((total, LANES), F32),
+                                        jax.ShapeDtypeStruct((2 * total, 2 * LANES), F32))
     valid_count, state_anom, radiance_anom, inv_noise, innovation = (pltpu.with_memory_space_constraint(x, pltpu.HBM) for x in (valid_count, state_anom, radiance_anom, inv_noise, innovation))
     gram, own_states, *factors = pl.pallas_call(
         functools.partial(gram_kernel, n_mem, n_chan, PARTS),

time: 18.5 us -> 18.5 us (level)
  no operation moved by 1% of the time
where the time goes in v4:
time: 18.5 us; the launch traced here: 18.3 us
  Pallas kernels  17.7 us (96%)
  between operations  0.64 us (3%)
    pallas_call x1, Pallas kernels, shards(): pl.pallas_call(functools.partial(gram_kernel, n_mem, n_chan, PARTS), out_...  15.6 us
    pallas_call x1, Pallas kernels, shards(): pl.pallas_call(functools.partial(solve_in_members if in_members else solv...  2.11 us

profile of v4, /device:TPU:0, one launch (start us, length us, event | category | flops | bytes accessed | tf_op | source)
XLA Modules:
  0.0 18.3 jit_solution(13152670982341840089)
XLA Ops:
  0.6 15.6 %shard_map.76 = (f32[40,128]{1,0:T(8,128)S(1)}, bf16[8,8,137]{2,1,0:T(8,128)(2,1)S(1)}, f32[64,128]{1,0:T(8,128)S(1)}, f32[128,256]{1,0:T(8,128)S(1)}) custom-call(s32[8]{0:T(128)} %count_hbm.1, bf16[8,8,137]{2,1,0:T(8,128)(2,1)} %state_hbm.1, bf16[8,8,2176]{2,1,0:T(8,128)(2,1)} %rad_hbm.1, f32[2176]{0:T(1024)} %noise_hbm.1, f32[8,2176]{1,0:T(8,128)} %innov_hbm.1), custom_call_target="tpu_custom_call" | custom-call | tf_op jit(solution)/shard_map/pallas_call | solution.py:385
  16.2 2.1 %shard_map.77 = (f32[137,1,137]{2,1,0:T(1,128)}, f32[1,137]{1,0:T(1,128)}, f32[1,137]{1,0:T(1,128)}) custom-call(f32[40,128]{1,0:T(8,128)S(1)} %get-tuple-element.10.gram_ref, bf16[8,8,137]{2,1,0:T(8,128)(2,1)S(1)} %get-tuple-element.11.states_ref, f32[64,128]{1,0:T(8,128)S(1)} %get-tuple-element.12.factor_ref, f32[128,256]{1,0:T(8,128)S(1)} %get-tuple-element.13.stacked_ref), custom_call_target="tpu_custom_call" | custom-call | tf_op jit(solution)/shard_map/pallas_call | solution.py:405

commit v5 on v4

--- a/solution.py
+++ b/solution.py
@@ -162,7 +162,7 @@
     slots = slab * width + lax.broadcasted_iota(jnp.int32, (1, width), 1)
     weight = jnp.where(slots < count[me], noise[...].reshape(1, width), 0.0)
     pull = weight * innov[pl.ds(me, 1), :]
-    pull = [part.astype(F32) for part in split2(pull)]
+    pull = [part.astype(F32) for part in split3(pull)]
 
     relays = []
     for i, copy in enumerate(far):
@@ -188,7 +188,7 @@
             hi = min(lo + step, stop)
             block = whole(mine, held, lo, hi)
             first, second = split2(block * weight[:, lo:hi])
-            tail = jnp.where(row == 0, pull[0][:, lo:hi], jnp.where(row == 1, pull[1][:, lo:hi], 0.0)).astype(BF16)
+            tail = sum(jnp.where(row == i, part[:, lo:hi], 0.0) for i, part in enumerate(pull)).astype(BF16)
             block = jnp.concatenate([block.astype(BF16)] * (columns // total), 0)
             acc += lax.dot_general(jnp.concatenate([first, second, tail], 0), block, (((1,), (1,)), ((), ())),
                                    preferred_element_type=F32)
@@ -197,7 +197,7 @@
         lane = lax.broadcasted_iota(jnp.int32, (height, columns), 1)
         square = jnp.where(lane < total, square[:height], square[height:])
     parts[slab, :height] = square
-    parts[slab, height:] = jnp.broadcast_to(acc[2 * total:2 * total + 1] + acc[2 * total + 1:2 * total + 2],
+    parts[slab, height:] = jnp.broadcast_to(sum(acc[2 * total + i:2 * total + i + 1] for i in range(len(pull))[::-1]),
                                             (SUB, columns))
     for k in range(1, n_chan):
         pltpu.make_async_remote_copy(
@@ -214,7 +214,9 @@
         tall = jnp.concatenate([anom, jnp.zeros((up(total, LANES) - total, anom.shape[1]), F32)], 0)
         square = lax.dot_general(anom.astype(BF16), tall.astype(BF16), (((1,), (1,)), ((), ())),
                                  preferred_element_type=F32)
-        factor = cholesky_rows(square, total)
+        rows = cholesky_rows(jnp.concatenate([square, anom], 1), total)
+        factor = rows[:, :LANES]
+        factor_refs[2][...] = rows[:, LANES:]
         factor_refs[0][...] = factor + pltpu.roll(factor, total, 1)
         stacked = stack_factor(factor, total)
         for i, tile in enumerate(stacked):
@@ -320,7 +322,7 @@
     inc_ref[...] = step.T[:1, :states]
 
 
-def solve_in_members(total, gram_ref, states_ref, factor_ref, stacked_ref, info_ref, grad_ref, inc_ref):
+def solve_in_members(total, gram_ref, states_ref, factor_ref, stacked_ref, basis_ref, info_ref, grad_ref, inc_ref):
     states = states_ref.shape[2]
     scale = 1.0 / (total - 1)
     rows, lanes = up(states, SUB), up(states, LANES)
@@ -357,9 +359,8 @@
     f0, f1, f2 = split3(jnp.broadcast_to(force, (2 * SUB, LANES)))
     gradient = (dots((f2, once), (jnp.where(left[:2 * SUB], f0, f1), twice.astype(BF16))) * scale)[:1]
     grad_ref[...] = gradient[:, :states]
-    moved = dots(*((m, twice.astype(BF16)) for m in (m2, m1, m0))) * (scale * scale * scale)
-    inc_ref[...] = (gradient - jnp.sum(jnp.concatenate([step] * (lanes // LANES), 1) * moved,
-                                       axis=0, keepdims=True))[:, :states]
+    inc_ref[...] = jnp.sum(jnp.concatenate([step * scale] * (lanes // LANES), 1) * basis_ref[...],
+                           axis=0, keepdims=True)[:, :states]
     across_states = twice.T[:rows].astype(BF16)
     outer = dots((across_states, jnp.concatenate([g2, jnp.zeros_like(g2)], 0)),
                  (across_states, jnp.concatenate([g0, g1], 0)))
@@ -380,7 +381,8 @@
     vmem, far = pl.BlockSpec(memory_space=pltpu.VMEM), pl.BlockSpec(memory_space=pltpu.HBM)
     dma = pltpu.SemaphoreType.DMA
     factor = () if not in_members else (jax.ShapeDtypeStruct((total, LANES), F32),
-                                        jax.ShapeDtypeStruct((2 * total, 2 * LANES), F32))
+                                        jax.ShapeDtypeStruct((2 * total, 2 * LANES), F32),
+                                        jax.ShapeDtypeStruct((total, up(states, LANES)), F32))
     valid_count, state_anom, radiance_anom, inv_noise, innovation = (pltpu.with_memory_space_constraint(x, pltpu.HBM) for x in (valid_count, state_anom, radiance_anom, inv_noise, innovation))
     gram, own_states, *factors = pl.pallas_call(
         functools.partial(gram_kernel, n_mem, n_chan, PARTS),

time: 18.5 us -> 18.5 us (level)
  no operation moved by 1% of the time
where the time goes in v5:
time: 18.5 us; the launch traced here: 18.3 us
  Pallas kernels  17.7 us (96%)
  between operations  0.64 us (3%)
    pallas_call x1, Pallas kernels, shards(): pl.pallas_call(functools.partial(gram_kernel, n_mem, n_chan, PARTS), out_...  15.6 us
    pallas_call x1, Pallas kernels, shards(): pl.pallas_call(functools.partial(solve_in_members if in_members else solv...  2.12 us

profile of v5, /device:TPU:0, one launch (start us, length us, event | category | flops | bytes accessed | tf_op | source)
XLA Modules:
  0.0 18.3 jit_solution(17045217400614419587)
XLA Ops:
  0.6 15.6 %shard_map.76 = (f32[40,128]{1,0:T(8,128)S(1)}, bf16[8,8,137]{2,1,0:T(8,128)(2,1)S(1)}, f32[64,128]{1,0:T(8,128)S(1)}, f32[128,256]{1,0:T(8,128)S(1)}, f32[64,256]{1,0:T(8,128)S(1)}) custom-call(s32[8]{0:T(128)} %count_hbm.1, bf16[8,8,137]{2,1,0:T(8,128)(2,1)} %state_hbm.1, bf16[8,8,2176]{2,1,0:T(8,128)(2,1)} %rad_hbm.1, f32[2176]{0:T(1024)} %noise_hbm.1, ...), custom_call_target="tpu_custom_call" | custom-call | tf_op jit(solution)/shard_map/pallas_call | solution.py:387
  16.2 2.1 %shard_map.77 = (f32[137,1,137]{2,1,0:T(1,128)}, f32[1,137]{1,0:T(1,128)}, f32[1,137]{1,0:T(1,128)}) custom-call(f32[40,128]{1,0:T(8,128)S(1)} %get-tuple-element.11.gram_ref, bf16[8,8,137]{2,1,0:T(8,128)(2,1)S(1)} %get-tuple-element.12.states_ref, f32[64,128]{1,0:T(8,128)S(1)} %get-tuple-element.13.factor_ref, ...), custom_call_target="tpu_custom_call" | custom-call | tf_op jit(solution)/shard_map/pallas_call | solution.py:407
